TPU v7x, 256 devices: a whole 4x4x8 slice. The times are simulated.
256 devices in a mesh: dp: 8 (over z_lo, core), vocab: 32 (over z_hi, x, y).
Axes of the slice: x: 4, y: 4, z: 8 (z_hi: 2, z_lo: 4; z = z_hi * 4 + z_lo), core: 2. Of those that a mesh axis runs over, the one named last changes fastest.
Arguments:
- policy_hidden: bfloat16 [1024, 4096], P('dp'), may hold values from -84 to 84
- policy_weight: bfloat16 [4096, 65536], P('dp', 'vocab'), may hold values from -0.09375 to 0.09375
- reference_hidden: bfloat16 [1024, 4096], P(('dp', 'vocab')), may hold values from -84 to 84
- reference_weight: bfloat16 [4096, 65536], P(None, ('dp', 'vocab')), may hold values from -0.09375 to 0.09375
- targets: int32 [1024], replicated, may hold values from 0 to 65535
- response_mask: int32 [1024], replicated, may hold values 0 or 1
- pair_index: int32 [32], replicated, may hold values from 0 to 31, each once
Outputs:
- hidden_grad: bfloat16 [1024, 4096], P('vocab', 'dp')
- weight_grad: bfloat16 [4096, 65536], P('dp', 'vocab')
- total_loss: float32 [], replicated
Inputs may be any that keep to these rules, and one draw needn't show every extreme that they name: `pair_index`: each number of 0 to 31 once; entries 2p and 2p + 1 are the chosen and the rejected sequence of pair p.
All inputs are finite; a program needn't handle non-finite values.
Results may differ from a plain program's by a relative error of at most 0.005.
The roundings to bfloat16 on the way count: a program that leaves them out, or rounds other values in their place, can miss the bound.
Values may be sent and summed in bfloat16 or wider, within the bound.
A program may use at most 128 MiB of HBM per device.

v0:
```python
import jax
import jax.numpy as jnp
from jax import lax
from jax.sharding import Mesh
from jax.sharding import PartitionSpec as P

SEQ_LEN = 32
DP = ("dp_0", "dp_1")
VOCAB = ("vocab_0", "vocab_1", "vocab_2")
DP_VOCAB = ("dp_0", "dp_1", "vocab_0", "vocab_1", "vocab_2")


beta = 0.1
loss_scale = 4096.0


def all_in_one(value, axis):
    leaves = jax.tree.leaves(value)
    order = sorted(range(len(leaves)), key=lambda k: -leaves[k].size)
    width = (1, *leaves[order[0]].shape)[-1]
    lines = [
        jnp.pad(leaves[k].reshape(-1), (0, -leaves[k].size % width)).reshape(-1, width)
        for k in order
    ]
    both, at, found = (lax.all_gather(jnp.concatenate(lines), axis), 0, {})
    for k, line in zip(order, lines):
        slab = both[:, at : at + len(line)].reshape(len(both), -1)
        found[k] = slab[:, : leaves[k].size].reshape(-1, *leaves[k].shape)
        at += len(line)
    numbers = iter(range(len(leaves)))
    return jax.tree.map(lambda _: found[next(numbers)], value)


def merged_by_axis(value, axes, combine):
    for axis in axes:
        pieces = all_in_one(value, axis)
        value = jax.tree.map(lambda part: part[0], pieces)
        for k in range(1, lax.axis_size(axis)):
            value = combine(value, jax.tree.map(lambda part: part[k], pieces))
    return value


def in_blocks(value, dim, peers):
    shape = value.shape
    tiles = value.reshape(*shape[:dim], peers, shape[dim] // peers, *shape[dim + 1 :])
    return jnp.moveaxis(tiles, dim, 0)


def sum_at_owner(value, axis, dim):
    peers = lax.axis_size(axis)
    tiles = lax.all_to_all(in_blocks(value, dim, peers), axis, 0, 0, tiled=True)
    return jnp.sum(tiles, axis=0)


def pair_terms(log_ratio, pair_index):
    chosen = pair_index[0::2]
    rejected = pair_index[1::2]
    margin = beta * (log_ratio[chosen] - log_ratio[rejected])
    pair_count = chosen.shape[0]
    total_loss = jnp.sum(jax.nn.softplus(-margin)) / pair_count
    weight = -beta * loss_scale * jax.nn.sigmoid(-margin) / pair_count
    numbers = jnp.arange(log_ratio.shape[0], dtype=jnp.int32)[:, None]
    factor = jnp.sum(
        jnp.where(numbers == chosen[None, :], weight[None, :], 0.0)
        - jnp.where(numbers == rejected[None, :], weight[None, :], 0.0),
        axis=1,
    )
    return (total_loss, factor)


def local_pick(logits, targets, offset, axis):
    column_ids = lax.broadcasted_iota(jnp.int32, logits.shape, axis)
    shifted = targets - offset
    wanted = shifted[:, None] if axis == 1 else shifted[None, :]
    return jnp.sum(jnp.where(column_ids == wanted, logits, 0.0), axis=axis)


def merge_pair(earlier, later):
    largest = jnp.maximum(earlier[0], later[0])
    exp_total = earlier[1] * jnp.exp(earlier[0] - largest) + later[1] * jnp.exp(later[0] - largest)
    return (largest, exp_total, earlier[2] + later[2])


def merge_heads(earlier, later):
    return merge_pair(earlier[0:3], later[0:3]) + merge_pair(earlier[3:6], later[3:6])


def local(
    policy_hidden,
    policy_weight,
    reference_hidden,
    reference_weight,
    targets,
    response_mask,
    pair_index,
):
    data_index = lax.axis_index(DP)
    vocab_index = lax.axis_index(VOCAB)
    vocab_devices = lax.axis_size(VOCAB)
    data_devices = lax.axis_size(DP)
    policy_width = policy_weight.shape[1]
    reference_width = reference_weight.shape[1]
    active = response_mask.astype(jnp.float32)
    columns = lax.all_to_all(policy_hidden, DP, split_axis=1, concat_axis=0, tiled=True)
    reference_logits = jnp.dot(
        lax.all_gather(reference_hidden, DP_VOCAB, axis=0, tiled=True),
        reference_weight,
        preferred_element_type=jnp.float32,
    )
    reference_offset = (data_index * vocab_devices + vocab_index) * reference_width
    reference_top = jnp.max(reference_logits, axis=1)
    reference_pick = local_pick(reference_logits, targets, reference_offset, 1)
    slice_width = policy_width // data_devices
    weight_block = policy_weight
    policy_logits = lax.psum_scatter(
        lax.dot_general(
            weight_block, columns, (((0,), (1,)), ((), ())), preferred_element_type=jnp.float32
        ),
        DP,
        scatter_dimension=0,
        tiled=True,
    )
    policy_offset = vocab_index * policy_width + data_index * slice_width
    policy_top = jnp.max(policy_logits, axis=0)
    policy_pick = local_pick(policy_logits, targets, policy_offset, 0)
    local_stats = (
        policy_top,
        jnp.sum(jnp.exp(policy_logits - policy_top[None, :]), axis=0),
        policy_pick,
        reference_top,
        jnp.sum(jnp.exp(reference_logits - reference_top[:, None]), axis=1),
        reference_pick,
    )
    merged = merged_by_axis(local_stats, DP_VOCAB, merge_heads)
    policy_total = merged[0] + jnp.log(merged[1])
    reference_logp = merged[5] - merged[3] - jnp.log(merged[4])
    log_ratio = jnp.sum(
        (active * (merged[2] - policy_total - reference_logp)).reshape(-1, SEQ_LEN), axis=1
    )
    total_loss, factor = pair_terms(log_ratio, pair_index)
    token_scale = active * jnp.repeat(factor, SEQ_LEN)
    row_ids = lax.broadcasted_iota(jnp.int32, policy_logits.shape, 0)
    onehot = (row_ids == (targets - policy_offset)[None, :]).astype(jnp.float32)
    logit_grad = (
        token_scale[None, :] * (onehot - jnp.exp(policy_logits - policy_total[None, :]))
    ).astype(jnp.bfloat16)
    segment = lax.all_gather(logit_grad, DP, axis=0, tiled=True)
    weight_block = policy_weight
    column_grad = lax.dot_general(
        columns, segment, (((0,), (1,)), ((), ())), preferred_element_type=jnp.float32
    )
    hidden_part = lax.dot_general(
        segment, weight_block, (((0,), (1,)), ((), ())), preferred_element_type=jnp.float32
    )
    weight_grad, hidden_part = (column_grad, hidden_part)
    hidden_grad = sum_at_owner(hidden_part, VOCAB, 0)
    return (hidden_grad.astype(jnp.bfloat16), weight_grad.astype(jnp.bfloat16), total_loss)


def solution(mesh):
    torus = Mesh(
        mesh.devices.reshape(4, 2, 2, 4, 4), ("dp_0", "dp_1", "vocab_0", "vocab_1", "vocab_2")
    )
    in_specs = (P(DP, None), P(DP, VOCAB), P(DP_VOCAB, None), P(None, DP_VOCAB), P(), P(), P())
    out_specs = (P(VOCAB, DP), P(DP, VOCAB), P())
    return jax.shard_map(local, mesh=torus, in_specs=in_specs, out_specs=out_specs, check_vma=False)
```

profile of v0, /device:TPU:38, one launch (start us, length us, event | category | flops | bytes accessed | tf_op | source)
XLA Modules:
  0.0 990.6 jit_solution(14023371967877538093)
XLA Ops:
  8.0 0.0 copy-start
  8.0 0.0 all-gather.16.cloned.1.call-start
  8.1 0.7 all-gather.16.cloned.1.call-update
  8.7 0.0 reduce-scatter.2.cloned.1.call-start
  8.8 2.3 copy.18
  11.1 30.3 %all_to_all.24 = bf16[128,8,512]{0,2,1:T(8,128)(2,1)S(1)} all-to-all(bf16[128,8,512]{0,2,1:T(8,128)(2,1)} %bitcast.453), channel_id=1, replica_groups=mesh['dp_0'=4,'dp_1'=2,'vocab_0'=2,'vocab_1'=4,'vocab_2'=4] {'dp_0','dp_1'}, dimensions={1} | all-to-all | bytes 2097152 | tf_op jit(solution)/shard_map/all_to_all | solution.py:104
  41.3 1.3 copy.19
  42.6 0.0 copy-done
  42.6 6.8 fusion.94
  49.5 0.0 copy-start.5
  49.5 0.0 copy-start.4
  49.5 0.0 reduce-scatter.2.cloned.1.call-update
  49.5 0.0 all-gather.14.cloned.1.call-start
  49.6 0.6 copy-done.5
  50.1 0.1 slice.613
  50.2 0.1 slice.516
  50.4 0.0 copy-done.4
  50.4 675.5 %all-gather.16.cloned.1.call-done = bf16[256,4,4096]{2,1,0:T(4,128)(2,1)} async-done(((bf16[1,4,4096]{2,1,0:T(4,128)(2,1)}), bf16[256,4,4096]{2,1,0:T(4,128)(2,1)}) %all-gather.16.cloned.1.call-update) | async-done | bytes 8388624 | tf_op jit(solution)/shard_map/all_gather | solution.py:106
  725.9 12.5 %reshape.1600 = bf16[1024,4096]{1,0:T(8,128)(2,1)} reshape(bf16[256,4,4096]{2,1,0:T(4,128)(2,1)} %all-gather.16.cloned.1.call-done) | data formatting | bytes 16777216
  738.4 6.4 fusion.93
  744.8 0.3 select_reduce_fusion
  745.1 0.0 copy-start.3
  745.1 0.0 reduce-scatter.2.cloned.1.call-done
  745.1 1.3 reduce_max.18
  746.4 0.0 copy-start.1
  746.4 1.6 select_reduce_fusion.1
  748.0 0.1 concatenate.15
  748.1 59.3 %all-gather.6 = f32[4,6,1024]{2,1,0:T(8,128)S(1)} all-gather(f32[1,6,1024]{2,1,0:T(8,128)S(1)} %bitcast.457), channel_id=2, replica_groups=mesh['dp_0'=4,'dp_1'=2,'vocab_0'=2,'vocab_1'=4,'vocab_2'=4] {'dp_0'}, dimensions={0}, use_global_device_ids=true | all-gather | bytes 122880 | tf_op jit(solution)/shard_map/all_gather | solution.py:25
  807.4 0.1 fusion.39
  807.5 0.1 concatenate.16
  807.6 1.9 all-gather.7
  809.5 0.1 concatenate.17
  809.5 8.5 all-gather.8
  818.1 0.1 concatenate.18
  818.1 21.7 %all-gather.9 = f32[4,6,1024]{2,1,0:T(8,128)S(1)} all-gather(f32[1,6,1024]{2,1,0:T(8,128)S(1)} %bitcast.460), channel_id=5, replica_groups=mesh['dp_0'=4,'dp_1'=2,'vocab_0'=2,'vocab_1'=4,'vocab_2'=4] {'vocab_1'}, dimensions={0}, use_global_device_ids=true | all-gather | bytes 122880 | tf_op jit(solution)/shard_map/all_gather | solution.py:25
  839.9 0.1 fusion.3
  840.0 0.1 concatenate.19
  840.0 12.1 %all-gather.10 = f32[4,6,1024]{2,1,0:T(8,128)S(1)} all-gather(f32[1,6,1024]{2,1,0:T(8,128)S(1)} %bitcast.461), channel_id=6, replica_groups=mesh['dp_0'=4,'dp_1'=2,'vocab_0'=2,'vocab_1'=4,'vocab_2'=4] {'vocab_2'}, dimensions={0}, use_global_device_ids=true | all-gather | bytes 122880 | tf_op jit(solution)/shard_map/all_gather | solution.py:25
  852.1 0.1 fusion.92
  852.2 0.0 copy-done.3
  852.2 0.1 reshape.1573
  852.3 0.1 reduce_sum.76
  852.4 0.7 gather_fusion.1
  853.1 0.7 gather_fusion
  853.8 0.6 fusion.83
  854.4 0.1 subtract_reduce_fusion
  854.5 0.1 broadcast_in_dim.51
  854.6 0.1 reshape.1574
  854.6 0.0 copy-done.1
  854.6 1.1 multiply_convert_fusion
  855.7 0.0 all-gather.14.cloned.1.call-update
  855.7 50.3 %all-gather.14.cloned.1.call-done = bf16[2048,1024]{1,0:T(8,128)(2,1)} async-done(((bf16[256,1024]{1,0:T(8,128)(2,1)}), bf16[2048,1024]{1,0:T(8,128)(2,1)}) %all-gather.14.cloned.1.call-update) | async-done | bytes 4194320 | tf_op jit(solution)/shard_map/all_gather | solution.py:147
  906.1 5.9 fusion.95
  912.0 0.0 copy-start.2
  912.0 13.1 %all-to-all-start.1 = ((f32[32,32,512]{2,1,0:T(8,128)}), f32[32,32,512]{2,1,0:T(8,128)}, u32[]{:S(2)}, u32[]{:S(2)}) async-start(f32[32,32,512]{2,1,0:T(8,128)} %bitcast.454), calls=%async_computation.2 | async-start | bytes 4194304 | tf_op jit(solution)/shard_map/all_to_all | solution.py:51
  925.8 0.0 copy-done.2
  925.8 5.9 fusion
  931.7 3.9 copy.20
  935.6 44.1 %all-to-all-done.1 = f32[32,32,512]{2,1,0:T(8,128)} async-done(((f32[32,32,512]{2,1,0:T(8,128)}), f32[32,32,512]{2,1,0:T(8,128)}, u32[]{:S(2)}, u32[]{:S(2)}) %all-to-all-start.1) | async-done | bytes 2097184 | tf_op jit(solution)/shard_map/all_to_all | solution.py:51
  979.7 2.4 reduce_sum.78
  (14 shorter events, 0.3 us)
Async XLA Ops:
  8.0 34.6 %copy-start = (bf16[512,2048]{1,0:T(8,128)(2,1)S(1)}, bf16[512,2048]{1,0:T(8,128)(2,1)}, u32[]{:S(2)}) copy-start(bf16[512,2048]{1,0:T(8,128)(2,1)} %param.8) | copy-start | bytes 6291460
  8.0 717.9 %all-gather.16.cloned.1.call-start = ((), (), s32[]{:S(2)}) async-start(), calls=%async_computation.5 | async-start | bytes 8421376 | tf_op jit(solution)/shard_map/all_gather | solution.py:106
  8.7 736.4 %reduce-scatter.2.cloned.1.call-start = ((), (), s32[]{:S(2)}) async-start(), calls=%async_computation.3 | async-start | bytes 9437184 | tf_op jit(solution)/shard_map/reduce_scatter | solution.py:115
  49.5 0.7 copy-start.5
  49.5 0.9 copy-start.4
  49.5 856.6 %all-gather.14.cloned.1.call-start = ((), (), s32[]{:S(2)}) async-start(), calls=%async_computation.4 | async-start | bytes 4718592 | tf_op jit(solution)/shard_map/all_gather | solution.py:147
  745.1 107.1 %copy-start.3 = (s32[1024]{0:T(1024)S(1)}, s32[1024]{0:T(1024)}, u32[]{:S(2)}) copy-start(s32[1024]{0:T(1024)} %param.12) | copy-start | bytes 12292
  746.4 108.2 %copy-start.1 = (f32[256,1024]{1,0:T(8,128)S(1)}, f32[256,1024]{1,0:T(8,128)}, u32[]{:S(2)}) copy-start(f32[256,1024]{1,0:T(8,128)} %reduce-scatter.2.cloned.1.call-done) | copy-start | bytes 3145732
  912.0 13.8 %copy-start.2 = (bf16[8,128,512]{2,1,0:T(8,128)(2,1)S(1)}, bf16[8,128,512]{2,1,0:T(8,128)(2,1)}, u32[]{:S(2)}) copy-start(bf16[8,128,512]{2,1,0:T(8,128)(2,1)} %copy.19) | copy-start | bytes 3145732
  912.0 67.7 %all-to-all-start.1 = ((f32[32,32,512]{2,1,0:T(8,128)}), f32[32,32,512]{2,1,0:T(8,128)}, u32[]{:S(2)}, u32[]{:S(2)}) async-start(f32[32,32,512]{2,1,0:T(8,128)} %bitcast.454), calls=%async_computation.2 | async-start | bytes 4194304 | tf_op jit(solution)/shard_map/all_to_all | solution.py:51
Sparse Core Ops, SparseCore 0:
  10.7 715.1 all-gather.15
Sparse Core Ops, SparseCore 1:
  49.6 93.9 reduce-scatter.1
  855.8 50.2 all-gather.13
where the time goes:
time: 991 us
  waiting for transfers between devices  771 us (78%)
  blocking collectives  134 us (14%)
  matrix products  25 us (3%)
  local copies, waits for them, and re-layouts  22.6 us (2%)
  between operations  17.5 us (2%)
  starting transfers between devices  13.3 us (1%)
    all_gather x1, waiting for transfers between devices, local(): lax.all_gather(reference_hidden, DP_VOCAB, axis=0, tiled=True)  675 us
    all_gather x5, blocking collectives, all_in_one(): both, at, found = (lax.all_gather(jnp.concatenate(lines), axis), 0, {})  103 us
    all_gather x1, waiting for transfers between devices, local(): segment = lax.all_gather(logit_grad, DP, axis=0, tiled=True)  50.3 us
    all_to_all x1, waiting for transfers between devices, sum_at_owner(): tiles = lax.all_to_all(in_blocks(value, dim, peers), axis, 0, 0, tiled=True)  44.1 us
    all_to_all x1, blocking collectives, local(): lax.all_to_all(policy_hidden, DP, split_axis=1, concat_axis=0, tiled=True)  30.3 us
  transfers between devices with their start and end apart: 4, of which 3 were waited for; matrix products, arithmetic and copies ran while one was open for 4% of the time, Pallas kernels for 0%

commit v1 on v0

--- a/solution.py
+++ b/solution.py
@@ -102,14 +102,22 @@
     reference_width = reference_weight.shape[1]
     active = response_mask.astype(jnp.float32)
     columns = lax.all_to_all(policy_hidden, DP, split_axis=1, concat_axis=0, tiled=True)
+    reference_rows = reference_hidden
+    for axis in ("dp_0", "vocab_0", "vocab_2", "vocab_1", "dp_1"):
+        reference_rows = lax.all_gather(reference_rows, axis, axis=0, tiled=True)
     reference_logits = jnp.dot(
-        lax.all_gather(reference_hidden, DP_VOCAB, axis=0, tiled=True),
+        reference_rows,
         reference_weight,
         preferred_element_type=jnp.float32,
     )
+    reference_targets = targets.reshape(4, 2, 2, 4, 4, 4).transpose(1, 3, 4, 2, 0, 5).reshape(-1)
+
+    def in_order(value):
+        return value.reshape(2, 4, 4, 2, 4, 4).transpose(4, 0, 3, 1, 2, 5).reshape(-1)
+
     reference_offset = (data_index * vocab_devices + vocab_index) * reference_width
     reference_top = jnp.max(reference_logits, axis=1)
-    reference_pick = local_pick(reference_logits, targets, reference_offset, 1)
+    reference_pick = local_pick(reference_logits, reference_targets, reference_offset, 1)
     slice_width = policy_width // data_devices
     weight_block = policy_weight
     policy_logits = lax.psum_scatter(
@@ -127,9 +135,9 @@
         policy_top,
         jnp.sum(jnp.exp(policy_logits - policy_top[None, :]), axis=0),
         policy_pick,
-        reference_top,
-        jnp.sum(jnp.exp(reference_logits - reference_top[:, None]), axis=1),
-        reference_pick,
+        in_order(reference_top),
+        in_order(jnp.sum(jnp.exp(reference_logits - reference_top[:, None]), axis=1)),
+        in_order(reference_pick),
     )
     merged = merged_by_axis(local_stats, DP_VOCAB, merge_heads)
     policy_total = merged[0] + jnp.log(merged[1])

time: 991 us -> 439 us (0.44)
  waiting for transfers between devices: 771 us -> 260 us
  blocking collectives: 134 us -> 103 us
  local copies, waits for them, and re-layouts: 22.6 us -> 11.9 us
    all_gather x1 -> x3, waiting for transfers between devices: 675 us -> 79.4 us  [local(): reference_rows = lax.all_gather(reference_rows, axis, axis=0, tiled=True)]
    reduce_scatter x1, waiting for transfers between devices: 0.03 us -> 84.9 us  [local(): lax.psum_scatter(lax.dot_general(weight_block, columns, (((0,), (1,)), ((...]
    all_gather x5, blocking collectives: 103 us -> 49 us  [all_in_one(): both, at, found = (lax.all_gather(jnp.concatenate(lines), axis), 0, {})]
    all_gather x0 -> x2, blocking collectives: none -> 24.6 us  [local(): reference_rows = lax.all_gather(reference_rows, axis, axis=0, tiled=True)]
    unnamed x15 -> x17, local copies, waits for them, and re-layouts: 19.3 us -> 6.99 us
  transfers between devices with their start and end apart: 4 -> 6, of which waited for: 3 -> 5; matrix products, arithmetic and copies ran while one was open for 4% -> 6% of each run, Pallas kernels for 0% -> 0%
where the time goes in v1:
time: 439 us; the launch traced here: 438 us
  waiting for transfers between devices  260 us (59%)
  blocking collectives  103 us (23%)
  matrix products  25 us (6%)
  between operations  17.2 us (4%)
  starting transfers between devices  13.3 us (3%)
  local copies, waits for them, and re-layouts  11.9 us (3%)
  other arithmetic  7.93 us (2%)
    reduce_scatter x1, waiting for transfers between devices, local(): lax.psum_scatter(lax.dot_general(weight_block, columns, (((0,), (1,)), ((...  84.9 us
    all_gather x3, waiting for transfers between devices, local(): reference_rows = lax.all_gather(reference_rows, axis, axis=0, tiled=True)  79.4 us
    all_gather x1, waiting for transfers between devices, local(): segment = lax.all_gather(logit_grad, DP, axis=0, tiled=True)  51.4 us
    all_gather x5, blocking collectives, all_in_one(): both, at, found = (lax.all_gather(jnp.concatenate(lines), axis), 0, {})  49 us
    all_to_all x1, waiting for transfers between devices, sum_at_owner(): tiles = lax.all_to_all(in_blocks(value, dim, peers), axis, 0, 0, tiled=True)  44.1 us
    all_to_all x1, blocking collectives, local(): lax.all_to_all(policy_hidden, DP, split_axis=1, concat_axis=0, tiled=True)  29.5 us
    all_gather x2, blocking collectives, local(): reference_rows = lax.all_gather(reference_rows, axis, axis=0, tiled=True)  24.6 us
    all_to_all x1, starting transfers between devices, sum_at_owner(): tiles = lax.all_to_all(in_blocks(value, dim, peers), axis, 0, 0, tiled=True)  13.1 us
  transfers between devices with their start and end apart: 6, of which 5 were waited for; matrix products, arithmetic and copies ran while one was open for 6% of the time, Pallas kernels for 0%

profile of v1, /device:TPU:38, one launch (start us, length us, event | category | flops | bytes accessed | tf_op | source)
XLA Modules:
  0.0 438.4 jit_solution(6761728711644219476)
XLA Ops:
  8.0 0.0 all-gather.16.cloned.1.call-start
  8.1 14.9 %all-gather.5 = bf16[4,4,4096]{2,1,0:T(4,128)(2,1)S(1)} all-gather(bf16[1,4,4096]{2,1,0:T(4,128)(2,1)} %bitcast.468), channel_id=1, replica_groups=mesh['dp_0'=4,'dp_1'=2,'vocab_0'=2,'vocab_1'=4,'vocab_2'=4] {'dp_0'}, dimensions={0}, use_global_device_ids=true | all-gather | bytes 163840 | tf_op jit(solution)/shard_map/all_gather | solution.py:107
  23.0 9.7 %all_gather.49 = bf16[32,4096]{1,0:T(8,128)(2,1)} all-gather(bf16[16,4096]{1,0:T(8,128)(2,1)S(1)} %reshape.1628), channel_id=1, replica_groups=mesh['dp_0'=4,'dp_1'=2,'vocab_0'=2,'vocab_1'=4,'vocab_2'=4] {'vocab_0'}, dimensions={0}, use_global_device_ids=true | all-gather | bytes 393216 | tf_op jit(solution)/shard_map/all_gather | solution.py:107
  32.7 0.0 all-gather.16.cloned.1.call-update
  32.8 0.0 all-gather.18.cloned.1.call-start
  32.8 28.1 %all-gather.16.cloned.1.call-done = bf16[128,4096]{1,0:T(8,128)(2,1)} async-done(((bf16[32,4096]{1,0:T(8,128)(2,1)}), bf16[128,4096]{1,0:T(8,128)(2,1)}) %all-gather.16.cloned.1.call-update) | async-done | bytes 1048592 | tf_op jit(solution)/shard_map/all_gather | solution.py:107
  60.9 0.0 all-gather.20.cloned.1.call-start
  61.0 51.3 %all-gather.18.cloned.1.call-done = bf16[512,4096]{1,0:T(8,128)(2,1)} async-done(((bf16[128,4096]{1,0:T(8,128)(2,1)}), bf16[512,4096]{1,0:T(8,128)(2,1)}) %all-gather.18.cloned.1.call-update) | async-done | bytes 4194320 | tf_op jit(solution)/shard_map/all_gather | solution.py:107
  112.3 0.0 reduce-scatter.2.cloned.1.call-start
  112.3 1.1 copy-done.2
  113.5 1.3 copy.26
  114.8 29.5 %all_to_all.24 = bf16[128,8,512]{0,2,1:T(8,128)(2,1)S(1)} all-to-all(bf16[128,8,512]{0,2,1:T(8,128)(2,1)} %bitcast.454), channel_id=1, replica_groups=mesh['dp_0'=4,'dp_1'=2,'vocab_0'=2,'vocab_1'=4,'vocab_2'=4] {'dp_0','dp_1'}, dimensions={1} | all-to-all | bytes 2097152 | tf_op jit(solution)/shard_map/all_to_all | solution.py:104
  144.3 1.3 copy.27
  145.6 6.8 %fusion.94 = f32[2048,1024]{1,0:T(8,128)} fusion(bf16[512,2048]{1,0:T(8,128)(2,1)S(1)} %copy-done, bf16[1024,512]{1,0:T(8,128)(2,1)} %bitcast.456), kind=kOutput, calls=%fused_computation.187 | convolution fusion | flops 2147483648 | bytes 11534336 | tf_op jit(solution)/shard_map/dot_general | solution.py:124
  152.5 0.0 reduce-scatter.2.cloned.1.call-update
  152.5 0.0 all-gather.22.cloned.1.call-start
  152.6 0.6 copy-done.6
  153.1 0.1 slice.613
  153.2 0.1 slice.516
  153.4 0.2 sub.464
  153.6 0.1 copy.30
  153.7 0.2 sub.466
  153.9 0.0 all-gather.20.cloned.1.call-done
  153.9 6.4 %fusion.93 = (f32[1024]{0:T(1024)S(1)}, f32[1024,256]{0,1:T(8,128)S(1)}) fusion(bf16[1024,4096]{1,0:T(8,128)(2,1)} %all-gather.20.cloned.1.call-done, bf16[4096,256]{1,0:T(8,128)(2,1)} %param.10), kind=kOutput, calls=%fused_computation.186 | convolution fusion | flops 2147744768 | bytes 11538432 | tf_op jit(solution)/shard_map/dot_general | solution.py:108
  160.3 0.2 reshape.1595
  160.5 0.3 select_reduce_fusion
  160.7 0.2 reshape.1599
  161.0 0.2 reshape.1600
  161.2 0.2 reshape.1596
  161.3 0.2 reshape.1597
  161.6 0.2 reshape.1598
  161.8 84.9 %reduce-scatter.2.cloned.1.call-done = f32[256,1024]{1,0:T(8,128)} async-done(((f32[2048,1024]{1,0:T(8,128)}), f32[256,1024]{1,0:T(8,128)}) %reduce-scatter.2.cloned.1.call-update) | async-done | bytes 1048592 | tf_op jit(solution)/shard_map/reduce_scatter | solution.py:123
  246.6 1.3 reduce_max.18
  248.0 1.6 select_reduce_fusion.1
  249.5 0.1 concatenate.15
  249.6 14.0 %all-gather.6 = f32[4,6,1024]{2,1,0:T(8,128)S(1)} all-gather(f32[1,6,1024]{2,1,0:T(8,128)S(1)} %bitcast.462), channel_id=2, replica_groups=mesh['dp_0'=4,'dp_1'=2,'vocab_0'=2,'vocab_1'=4,'vocab_2'=4] {'dp_0'}, dimensions={0}, use_global_device_ids=true | all-gather | bytes 122880 | tf_op jit(solution)/shard_map/all_gather | solution.py:25
  263.7 0.1 fusion.39
  263.8 0.1 concatenate.16
  263.8 1.9 all-gather.7
  265.7 0.1 concatenate.17
  265.8 8.5 %all-gather.8 = f32[2,6,1024]{2,1,0:T(8,128)S(1)} all-gather(f32[1,6,1024]{2,1,0:T(8,128)S(1)} %bitcast.464), channel_id=4, replica_groups=mesh['dp_0'=4,'dp_1'=2,'vocab_0'=2,'vocab_1'=4,'vocab_2'=4] {'vocab_0'}, dimensions={0}, use_global_device_ids=true | all-gather | bytes 73728 | tf_op jit(solution)/shard_map/all_gather | solution.py:25
  274.4 0.1 concatenate.18
  274.4 12.0 %all-gather.9 = f32[4,6,1024]{2,1,0:T(8,128)S(1)} all-gather(f32[1,6,1024]{2,1,0:T(8,128)S(1)} %bitcast.465), channel_id=5, replica_groups=mesh['dp_0'=4,'dp_1'=2,'vocab_0'=2,'vocab_1'=4,'vocab_2'=4] {'vocab_1'}, dimensions={0}, use_global_device_ids=true | all-gather | bytes 122880 | tf_op jit(solution)/shard_map/all_gather | solution.py:25
  286.4 0.1 fusion.3
  286.5 0.1 concatenate.19
  286.6 12.6 %all-gather.10 = f32[4,6,1024]{2,1,0:T(8,128)S(1)} all-gather(f32[1,6,1024]{2,1,0:T(8,128)S(1)} %bitcast.466), channel_id=6, replica_groups=mesh['dp_0'=4,'dp_1'=2,'vocab_0'=2,'vocab_1'=4,'vocab_2'=4] {'vocab_2'}, dimensions={0}, use_global_device_ids=true | all-gather | bytes 122880 | tf_op jit(solution)/shard_map/all_gather | solution.py:25
  299.2 0.1 fusion.92
  299.3 0.1 reshape.1601
  299.4 0.1 reduce_sum.76
  299.5 0.7 gather_fusion.1
  300.2 0.7 gather_fusion
  300.8 0.6 fusion.83
  301.5 0.1 subtract_reduce_fusion
  301.6 0.1 broadcast_in_dim.51
  301.6 0.1 reshape.1602
  301.7 1.1 multiply_convert_fusion
  302.8 0.0 all-gather.22.cloned.1.call-update
  302.8 51.4 %all-gather.22.cloned.1.call-done = bf16[2048,1024]{1,0:T(8,128)(2,1)} async-done(((bf16[256,1024]{1,0:T(8,128)(2,1)}), bf16[2048,1024]{1,0:T(8,128)(2,1)}) %all-gather.22.cloned.1.call-update) | async-done | bytes 4194320 | tf_op jit(solution)/shard_map/all_gather | solution.py:155
  354.2 5.9 %fusion.95 = f32[1024,512]{1,0:T(8,128)} fusion(bf16[2048,1024]{1,0:T(8,128)(2,1)} %all-gather.22.cloned.1.call-done, bf16[512,2048]{1,0:T(8,128)(2,1)S(1)} %copy-done), kind=kOutput, calls=%fused_computation.188 | convolution fusion | flops 2147483648 | bytes 8388608 | tf_op jit(solution)/shard_map/dot_general | solution.py:160
  360.1 13.1 %all-to-all-start.1 = ((f32[32,32,512]{2,1,0:T(8,128)}), f32[32,32,512]{2,1,0:T(8,128)}, u32[]{:S(2)}, u32[]{:S(2)}) async-start(f32[32,32,512]{2,1,0:T(8,128)} %bitcast.455), calls=%async_computation.2 | async-start | bytes 4194304 | tf_op jit(solution)/shard_map/all_to_all | solution.py:51
  373.9 5.9 %fusion = bf16[512,2048]{0,1:T(8,128)(2,1)} fusion(bf16[2048,1024]{1,0:T(8,128)(2,1)} %all-gather.22.cloned.1.call-done, bf16[1024,512]{1,0:T(8,128)(2,1)S(1)} %bitcast.457), kind=kOutput, calls=%fused_computation.3 | convolution fusion | flops 2148532224 | bytes 7340032 | tf_op jit(solution)/shard_map/dot_general | solution.py:157
  379.8 3.9 copy.32
  383.7 44.1 %all-to-all-done.1 = f32[32,32,512]{2,1,0:T(8,128)} async-done(((f32[32,32,512]{2,1,0:T(8,128)}), f32[32,32,512]{2,1,0:T(8,128)}, u32[]{:S(2)}, u32[]{:S(2)}) %all-to-all-start.1) | async-done | bytes 2097184 | tf_op jit(solution)/shard_map/all_to_all | solution.py:51
  427.8 2.4 reduce_sum.78
  (32 shorter events, 0.5 us)
Async XLA Ops:
  8.0 137.6 %copy-start = (bf16[512,2048]{1,0:T(8,128)(2,1)S(1)}, bf16[512,2048]{1,0:T(8,128)(2,1)}, u32[]{:S(2)}) copy-start(bf16[512,2048]{1,0:T(8,128)(2,1)} %param.8) | copy-start | bytes 6291460
  8.0 52.9 %all-gather.16.cloned.1.call-start = ((), (), s32[]{:S(2)}) async-start(), calls=%async_computation.4 | async-start | bytes 1310720 | tf_op jit(solution)/shard_map/all_gather | solution.py:107
  32.8 79.5 %all-gather.18.cloned.1.call-start = ((), (), s32[]{:S(2)}) async-start(), calls=%async_computation.5 | async-start | bytes 5242880 | tf_op jit(solution)/shard_map/all_gather | solution.py:107
  60.9 93.0 %all-gather.20.cloned.1.call-start = ((), (), s32[]{:S(2)}) async-start(), calls=%async_computation.6 | async-start | bytes 12582912 | tf_op jit(solution)/shard_map/all_gather | solution.py:107
  112.3 1.2 copy-start.2
  112.3 134.4 %reduce-scatter.2.cloned.1.call-start = ((), (), s32[]{:S(2)}) async-start(), calls=%async_computation.3 | async-start | bytes 9437184 | tf_op jit(solution)/shard_map/reduce_scatter | solution.py:123
  152.5 0.7 copy-start.6
  152.5 0.9 copy-start.5
  152.5 201.7 %all-gather.22.cloned.1.call-start = ((), (), s32[]{:S(2)}) async-start(), calls=%async_computation.7 | async-start | bytes 4718592 | tf_op jit(solution)/shard_map/all_gather | solution.py:155
  161.5 137.7 %copy-start.4 = (s32[1024]{0:T(1024)S(1)}, s32[1024]{0:T(1024)}, u32[]{:S(2)}) copy-start(s32[1024]{0:T(1024)} %param.12) | copy-start | bytes 12292
  247.9 53.8 %copy-start.1 = (f32[256,1024]{1,0:T(8,128)S(1)}, f32[256,1024]{1,0:T(8,128)}, u32[]{:S(2)}) copy-start(f32[256,1024]{1,0:T(8,128)} %reduce-scatter.2.cloned.1.call-done) | copy-start | bytes 3145732
  360.1 13.8 %copy-start.3 = (bf16[8,128,512]{2,1,0:T(8,128)(2,1)S(1)}, bf16[8,128,512]{2,1,0:T(8,128)(2,1)}, u32[]{:S(2)}) copy-start(bf16[8,128,512]{2,1,0:T(8,128)(2,1)} %copy.27) | copy-start | bytes 3145732
  360.1 67.7 %all-to-all-start.1 = ((f32[32,32,512]{2,1,0:T(8,128)}), f32[32,32,512]{2,1,0:T(8,128)}, u32[]{:S(2)}, u32[]{:S(2)}) async-start(f32[32,32,512]{2,1,0:T(8,128)} %bitcast.455), calls=%async_computation.2 | async-start | bytes 4194304 | tf_op jit(solution)/shard_map/all_to_all | solution.py:51
Sparse Core Ops, SparseCore 0:
  32.9 27.9 all-gather.15
  62.7 49.5 all-gather.17
  114.1 27.0 all-gather.19
Sparse Core Ops, SparseCore 1:
  152.6 94.0 reduce-scatter.1
  302.9 51.2 all-gather.21
